TPU v7x, 32 devices: a whole 2x2x4 slice. The times are simulated.
32 devices in a mesh: owner: 4 (over y, core), rows: 8 (over z, x).
Axes of the slice: x: 2, y: 2, z: 4, core: 2. Of those that a mesh axis runs over, the one named last changes fastest.
Arguments:
- w_down: float32 [16, 6400, 4096], P('owner', None, 'rows'), may hold values from -0.109375 to 0.109375
- avg_down: bfloat16 [16, 6400, 4096], P('owner', None, 'rows'), may hold values from -0.0390625 to 0.0390625
- router_weight: float32 [4096, 16], P('rows', 'owner'), may hold values from -0.09375 to 0.09375
- router_gain: float32 [4096], P('rows'), may hold values from 0.25 to 1.75
Outputs:
- serve_down: bfloat16 [16, 6400, 4096], P('owner', 'rows')
- scale_down: float32 [16, 6400], P('owner', 'rows')
- serve_router: bfloat16 [4096, 16], replicated
All inputs are finite; a program needn't handle non-finite values.
Results may differ from a plain program's by a relative error of at most 0.0085.
Values may be sent and summed in bfloat16 or wider, within the bound.
A program may use at most 256 MiB of HBM per device.

v0:
```python
import jax
import jax.numpy as jnp
from jax import lax
from jax.sharding import PartitionSpec as P


def local(w_down, avg_down, router_weight, router_gain):
    fresh_down = w_down + avg_down.astype(jnp.float32)
    total_down = lax.psum(
        jnp.sum(fresh_down * fresh_down, axis=2).astype(jnp.bfloat16), "rows"
    ).astype(jnp.float32)
    scale_down = jnp.sqrt(total_down)
    narrow_down = (fresh_down / jnp.expand_dims(scale_down, 2)).astype(jnp.bfloat16)
    serve_down = lax.all_to_all(narrow_down, "rows", split_axis=1, concat_axis=2, tiled=True)
    scale_down = lax.dynamic_slice_in_dim(
        scale_down, lax.axis_index("rows") * serve_down.shape[1], serve_down.shape[1], axis=1
    )
    part_router = (router_weight * router_gain[:, None]).astype(jnp.bfloat16)
    row_router = lax.all_gather(part_router, "rows", axis=0, tiled=True)
    serve_router = lax.all_gather(row_router, "owner", axis=1, tiled=True)
    return (serve_down, scale_down, serve_router)


def solution(mesh):
    return jax.shard_map(
        local,
        mesh=mesh,
        in_specs=(
            P("owner", None, "rows"),
            P("owner", None, "rows"),
            P("rows", "owner"),
            P("rows"),
        ),
        out_specs=(P("owner", "rows", None), P("owner", "rows"), P()),
        check_vma=False,
    )
```

profile of v0, /device:TPU:0, one launch (start us, length us, event | category | flops | bytes accessed | tf_op | source)
XLA Modules:
  0.0 826.9 jit_solution(7862156734528137198)
XLA Ops:
  0.6 24.2 %multiply_reduce_fusion = bf16[4,6400]{1,0:T(4,128)(2,1)S(1)} fusion(f32[4,6400,512]{2,1,0:T(8,128)} %param.4, bf16[4,6400,512]{2,1,0:T(8,128)(2,1)} %param.5), kind=kLoop, calls=%fused_computation.1 | loop fusion | flops 52403200 | bytes 78694400 | tf_op jit(solution)/shard_map/reduce_sum | solution.py:10
  24.9 0.9 copy.21
  25.8 83.5 %psum.7 = bf16[4,6400]{0,1:T(8,128)(2,1)} all-reduce(bf16[4,6400]{0,1:T(8,128)(2,1)S(1)} %copy.21), channel_id=1, replica_groups=mesh['owner'=4,'rows'=8] {'rows'}, use_global_device_ids=true, to_apply=%region_1.0 | all-reduce | flops 25600 | bytes 102400 | tf_op jit(solution)/shard_map/psum | solution.py:9
  109.3 2.3 convert_sqrt_fusion
  111.6 1.2 copy.17
  112.8 34.3 %divide_convert_fusion = bf16[4,6400,512]{2,1,0:T(8,128)(2,1)} fusion(f32[4,6400,512]{2,1,0:T(8,128)} %param.4, bf16[4,6400,512]{2,1,0:T(8,128)(2,1)} %param.5, f32[4,6400]{1,0:T(4,128)S(1)} %copy.17), kind=kLoop, calls=%fused_computation | loop fusion | flops 52428800 | bytes 104960000 | tf_op jit(solution)/shard_map/convert_element_type | solution.py:13
  147.1 33.4 %copy.18 = bf16[4,6400,512]{2,0,1:T(4,128)(2,1)} copy(bf16[4,6400,512]{2,1,0:T(8,128)(2,1)} %divide_convert_fusion) | data formatting | bytes 52428800 | tf_op jit(solution)/shard_map/convert_element_type | solution.py:13
  180.5 0.0 copy-start
  180.5 0.0 copy-start.1
  180.5 6.6 all-to-all-start
  187.2 0.8 constant_dynamic-slice_fusion
  187.9 1.8 copy.20
  189.7 0.0 copy-done
  189.7 0.0 copy-done.1
  189.7 573.7 %all_gather.6 = bf16[4096,4]{0,1:T(4,128)(2,1)S(1)} all-gather(bf16[512,4]{0,1:T(4,128)(2,1)S(1)} %multiply_convert_fusion), channel_id=1, replica_groups=mesh['owner'=4,'rows'=8] {'rows'}, dimensions={0}, use_global_device_ids=true | all-gather | bytes 36864 | tf_op jit(solution)/shard_map/all_gather | solution.py:19
  763.4 5.4 all-gather
  768.8 0.7 reshape.9
  769.5 0.0 all-to-all-done
  769.5 18.2 %copy.19 = bf16[4,800,8,512]{3,2,1,0:T(8,128)(2,1)} copy(bf16[4,800,8,512]{3,0,1,2:T(4,128)(2,1)} %bitcast.1) | data formatting | bytes 52428800 | tf_op jit(solution)/shard_map/all_to_all | solution.py:14
  787.7 39.2 %all_to_all.16 = bf16[4,800,4096]{2,1,0:T(8,128)(2,1)} reshape(bf16[4,800,8,512]{3,2,1,0:T(8,128)(2,1)} %copy.19) | data formatting | bytes 52428800 | tf_op jit(solution)/shard_map/all_to_all | solution.py:14
  (1 shorter events, 0.0 us)
Async XLA Ops:
  180.5 9.2 %copy-start = (f32[512,4]{0,1:T(4,128)S(1)}, f32[512,4]{0,1:T(4,128)}, u32[]{:S(2)}) copy-start(f32[512,4]{0,1:T(4,128)} %param.6) | copy-start | bytes 24580
  180.5 9.2 %copy-start.1 = (f32[512]{0:T(512)S(1)}, f32[512]{0:T(512)}, u32[]{:S(2)}) copy-start(f32[512]{0:T(512)} %param.7) | copy-start | bytes 6148
  180.5 589.0 %all-to-all-start = ((bf16[4,6400,512]{2,0,1:T(4,128)(2,1)}), bf16[4,6400,512]{2,0,1:T(4,128)(2,1)}, u32[]{:S(2)}, u32[]{:S(2)}) async-start(bf16[4,6400,512]{2,0,1:T(4,128)(2,1)} %copy.18), calls=%async_computation | async-start | bytes 52428800 | tf_op jit(solution)/shard_map/all_to_all | solution.py:14
where the time goes:
time: 828 us; the launch traced here: 827 us
  blocking collectives  663 us (80%)
  local copies, waits for them, and re-layouts  96.2 us (12%)
  other arithmetic  60.8 us (7%)
    all_gather x1, blocking collectives, local(): row_router = lax.all_gather(part_router, 'rows', axis=0, tiled=True)  574 us
    psum x1, blocking collectives, local(): lax.psum(jnp.sum(fresh_down * fresh_down, axis=2).astype(jnp.bfloat16), '...  83.5 us
    all_to_all x2, local copies, waits for them, and re-layouts, local(): lax.all_to_all(narrow_down, 'rows', split_axis=1, concat_axis=2, tiled=True)  57.4 us
    convert_element_type x1, other arithmetic, local(): (fresh_down / jnp.expand_dims(scale_down, 2)).astype(jnp.bfloat16)  34.3 us
    convert_element_type x1, local copies, waits for them, and re-layouts, local(): (fresh_down / jnp.expand_dims(scale_down, 2)).astype(jnp.bfloat16)  33.4 us
    reduce_sum x1, other arithmetic, local(): jnp.sum(fresh_down * fresh_down, axis=2).astype(jnp.bfloat16)  24.2 us
  transfers between devices with their start and end apart: 1, of which 0 were waited for; matrix products, arithmetic and copies ran while one was open for 0% of the time, Pallas kernels for 0%

commit v1 on v0

--- a/solution.py
+++ b/solution.py
@@ -1,7 +1,18 @@
+import functools
 import jax
 import jax.numpy as jnp
 from jax import lax
 from jax.sharding import PartitionSpec as P
+
+
+def arrange_blocks_by_axis(mine, join_dim, dim_i):
+    s_next = jax.lax.axis_size("rows")
+    met_up = jnp.split(mine, s_next, join_dim)
+    then = jnp.concatenate(jax.lax.all_to_all(jnp.stack(met_up, axis=0), "rows", 0, 0), dim_i)
+    return then
+
+
+assign_sources_all = functools.partial(arrange_blocks_by_axis, join_dim=1, dim_i=2)
 
 
 def local(w_down, avg_down, router_weight, router_gain):
@@ -11,7 +22,7 @@
     ).astype(jnp.float32)
     scale_down = jnp.sqrt(total_down)
     narrow_down = (fresh_down / jnp.expand_dims(scale_down, 2)).astype(jnp.bfloat16)
-    serve_down = lax.all_to_all(narrow_down, "rows", split_axis=1, concat_axis=2, tiled=True)
+    serve_down = assign_sources_all(narrow_down)
     scale_down = lax.dynamic_slice_in_dim(
         scale_down, lax.axis_index("rows") * serve_down.shape[1], serve_down.shape[1], axis=1
     )

time: 828 us -> 739 us (0.89)
  local copies, waits for them, and re-layouts: 96.2 us -> 49.8 us
  blocking collectives: 663 us -> 623 us
    all_to_all x2 -> x0, local copies, waits for them, and re-layouts: 57.4 us -> none  [local(): lax.all_to_all(narrow_down, 'rows', split_axis=1, concat_axis=2, tiled=True)]
    psum x1, blocking collectives: 83.5 us -> 39.3 us  [local(): lax.psum(jnp.sum(fresh_down * fresh_down, axis=2).astype(jnp.bfloat16), '...]
    convert_element_type x1 -> x0, local copies, waits for them, and re-layouts: 33.4 us -> none  [local(): (fresh_down / jnp.expand_dims(scale_down, 2)).astype(jnp.bfloat16)]
    unnamed x7 -> x12, local copies, waits for them, and re-layouts: 3.4 us -> 27.5 us
    reshape x0 -> x1, local copies, waits for them, and re-layouts: none -> 17.9 us  [arrange_blocks_by_axis(): jnp.concatenate(jax.lax.all_to_all(jnp.stack(met_up, axis=0), 'rows', 0,...]
where the time goes in v1:
time: 739 us
  blocking collectives  623 us (84%)
  other arithmetic  58.6 us (8%)
  local copies, waits for them, and re-layouts  49.8 us (7%)
    all_gather x1, blocking collectives, local(): row_router = lax.all_gather(part_router, 'rows', axis=0, tiled=True)  578 us
    psum x1, blocking collectives, local(): lax.psum(jnp.sum(fresh_down * fresh_down, axis=2).astype(jnp.bfloat16), '...  39.3 us
    convert_element_type x1, other arithmetic, local(): (fresh_down / jnp.expand_dims(scale_down, 2)).astype(jnp.bfloat16)  34.3 us
    unnamed x12, local copies, waits for them, and re-layouts  27.5 us
    reduce_sum x1, other arithmetic, local(): jnp.sum(fresh_down * fresh_down, axis=2).astype(jnp.bfloat16)  24.2 us
    reshape x1, local copies, waits for them, and re-layouts, arrange_blocks_by_axis(): jnp.concatenate(jax.lax.all_to_all(jnp.stack(met_up, axis=0), 'rows', 0,...  17.9 us
  transfers between devices with their start and end apart: 1, of which 0 were waited for; matrix products, arithmetic and copies ran while one was open for 0% of the time, Pallas kernels for 0%

profile of v1, /device:TPU:0, one launch (start us, length us, event | category | flops | bytes accessed | tf_op | source)
XLA Modules:
  0.0 738.6 jit_solution(8709787585122454427)
XLA Ops:
  0.6 24.2 %multiply_reduce_fusion = bf16[4,6400]{1,0:T(4,128)(2,1)S(1)} fusion(f32[4,6400,512]{2,1,0:T(8,128)} %param.4, bf16[4,6400,512]{2,1,0:T(8,128)(2,1)} %param.5), kind=kLoop, calls=%fused_computation.1 | loop fusion | flops 52403200 | bytes 78694400 | tf_op jit(solution)/shard_map/reduce_sum | solution.py:21
  24.9 39.3 %psum.7 = bf16[4,6400]{1,0:T(4,128)(2,1)S(1)} all-reduce(bf16[4,6400]{1,0:T(4,128)(2,1)S(1)} %multiply_reduce_fusion), channel_id=1, replica_groups=mesh['owner'=4,'rows'=8] {'rows'}, use_global_device_ids=true, to_apply=%region_1.0 | all-reduce | flops 25600 | bytes 102400 | tf_op jit(solution)/shard_map/psum | solution.py:20
  64.2 0.1 convert_sqrt_fusion
  64.3 34.3 %divide_convert_fusion = bf16[4,6400,512]{2,1,0:T(8,128)(2,1)} fusion(f32[4,6400,512]{2,1,0:T(8,128)} %param.4, bf16[4,6400,512]{2,1,0:T(8,128)(2,1)} %param.5, f32[4,6400]{1,0:T(4,128)S(1)} %convert_sqrt_fusion), kind=kLoop, calls=%fused_computation | loop fusion | flops 52428800 | bytes 104960000 | tf_op jit(solution)/shard_map/convert_element_type | solution.py:24
  98.5 3.8 fusion.7
  102.4 3.8 fusion.6
  106.2 3.8 fusion.5
  110.0 3.8 fusion.4
  113.8 3.9 fusion.3
  117.7 3.8 fusion.2
  121.5 3.8 fusion.1
  125.3 3.8 fusion
  129.1 0.0 copy-start
  129.1 0.0 copy-start.1
  129.1 6.6 all-to-all-start
  135.8 0.0 copy-done
  135.8 0.0 copy-done.1
  135.8 578.1 %all_gather.6 = bf16[4096,4]{0,1:T(4,128)(2,1)S(1)} all-gather(bf16[512,4]{0,1:T(4,128)(2,1)S(1)} %multiply_convert_fusion), channel_id=1, replica_groups=mesh['owner'=4,'rows'=8] {'rows'}, dimensions={0}, use_global_device_ids=true | all-gather | bytes 36864 | tf_op jit(solution)/shard_map/all_gather | solution.py:30
  714.0 5.4 all-gather
  719.4 0.7 reshape.17
  720.1 0.7 constant_dynamic-slice_fusion
  720.7 0.0 all-to-all-done
  720.7 17.9 %copy.9 = bf16[8,4,100,8,512]{4,3,0,2,1:T(8,128)(2,1)} copy(bf16[8,4,100,8,512]{4,3,2,1,0:T(8,128)(2,1)} %bitcast.13) | data formatting | bytes 52428800 | tf_op jit(solution)/shard_map/reshape | solution.py:11
  (1 shorter events, 0.0 us)
Async XLA Ops:
  129.1 6.6 copy-start
  129.1 6.7 copy-start.1
  129.1 591.6 %all-to-all-start = ((bf16[8,4,800,512]{3,2,1,0:T(8,128)(2,1)}), bf16[8,4,800,512]{3,2,1,0:T(8,128)(2,1)}, u32[]{:S(2)}, u32[]{:S(2)}) async-start(bf16[8,4,800,512]{3,2,1,0:T(8,128)(2,1)} %fusion), calls=%async_computation | async-start | bytes 52428800 | tf_op jit(solution)/shard_map/all_to_all | solution.py:11
